TPU v7x, 512 devices: a whole 4x4x16 slice. The times are simulated.
512 devices in a mesh: grp: 16 (over z), dp: 32 (over x, y, core).
Axes of the slice: x: 4, y: 4, z: 16, core: 2. Of those that a mesh axis runs over, the one named last changes fastest.
Arguments:
- tokens: bfloat16 [65536, 3584], P(('grp', 'dp')), may hold values from -120 to 120, as said below
- lengths: int32 [512, 4], P(('grp', 'dp')), may hold values from 0 to 128, as said below
- dest: int32 [512, 4], P(('grp', 'dp')), may hold values from -1 to 15, as said below
- gain: float32 [3584], replicated, may hold values from 0.5 to 1.5
- weight: bfloat16 [3584, 10240], P('dp', 'grp'), may hold values from -0.09375 to 0.09375
Outputs:
- projected: bfloat16 [32768, 10240], P('dp', 'grp')
Inputs may be any that keep to these rules, and one draw needn't show every extreme that they name: The tokens of one row have a common scale, and so have those of one feature. A device's live rows are the sum of its lengths; rows after them are padding. Within the devices sharing a dp index, live rows fill ceil(live rows / 32) blocks on each device and 32 blocks in all. dest is -1 exactly for a device's blocks past its live rows and an owner along grp otherwise. Within the devices sharing a dp index, every owner receives exactly 2 blocks and no device sends more than 1 block to one owner.
All inputs are finite; a program needn't handle non-finite values.
Results may differ from a plain program's by a relative error of at most 0.0049.
Values may be sent and summed in bfloat16 or wider, within the bound.
No kernel may reach another device: no remote copies, remote signals or barrier semaphores. Data moves between devices by JAX's collectives and lax.ppermute only.
A program may use at most 64 MiB of HBM per device.

v0:
```python
import jax
import jax.numpy as jnp
from jax import lax
from jax.sharding import PartitionSpec as P

BLK = 32
OWN_BLK = 2
EPS = 1e-06


def in_one_piece(arrays, axis, dim, along):
    widths = [a.shape[along] for a in arrays]
    both = jnp.concatenate(arrays, axis=along)
    result = lax.all_gather(both, axis, axis=dim, tiled=True)
    return tuple(jnp.split(result, [sum(widths[:k]) for k in range(1, len(widths))], axis=along))


def group_layout(dest_all, own_blocks):
    groups, slots_in = dest_all.shape
    flat_dest = dest_all.reshape(-1)
    flat_index = jnp.arange(groups * slots_in, dtype=jnp.int32)
    earlier = flat_index[None, :] < flat_index[:, None]
    same_dest = flat_dest[:, None] == flat_dest[None, :]
    source = flat_index // slots_in
    owner_rank = jnp.sum((same_dest & earlier).astype(jnp.int32), axis=1)
    pair_rank = jnp.sum(
        (same_dest & earlier & (source[:, None] == source[None, :])).astype(jnp.int32), axis=1
    )
    matches = (flat_dest[:, None, None] == jnp.arange(groups, dtype=jnp.int32)[None, :, None]) & (
        owner_rank[:, None, None] == jnp.arange(own_blocks, dtype=jnp.int32)[None, None, :]
    )
    picked = jnp.sum(jnp.where(matches, flat_index[:, None, None], 0), axis=0)
    return (picked, pair_rank)


def local_onehot(lens_row, count):
    doc_ends = jnp.cumsum(lens_row)
    position = jnp.arange(count, dtype=jnp.int32)
    doc_index = jnp.sum((position[:, None] >= doc_ends[None, :]).astype(jnp.int32), axis=1)
    is_live = position < doc_ends[-1]
    return (
        doc_index[:, None] == jnp.arange(lens_row.shape[0], dtype=jnp.int32)[None, :]
    ) & is_live[:, None]


def doc_squares(rows, onehot):
    widened = rows.astype(jnp.float32)
    square = jnp.sum(widened * widened, axis=1)
    return jnp.sum(jnp.where(onehot, square[:, None], 0.0), axis=0)


def apply_scale(rows, onehot, totals, lens_flat, gain):
    features = rows.shape[1]
    mean_square = totals / (jnp.maximum(lens_flat, 1).astype(jnp.float32) * features)
    inverse = lax.rsqrt(mean_square + EPS)
    scale = jnp.sum(jnp.where(onehot, inverse[None, :], 0.0), axis=1)
    return (rows.astype(jnp.float32) * scale[:, None] * gain[None, :]).astype(jnp.bfloat16)


def fold_rows(rows_all, weight):
    return jnp.dot(
        rows_all,
        lax.all_gather(weight, "dp", axis=0, tiled=True),
        preferred_element_type=jnp.float32,
    ).astype(jnp.bfloat16)


def per_device(tokens, lengths, dest, gain, weight):
    groups = lax.axis_size("grp")
    slots_in = 2 * OWN_BLK
    features = tokens.shape[1]
    pair_most = max(1, (slots_in + groups - 1) // groups)
    lens_all, dest_all = in_one_piece((lengths, dest), "grp", 0, 1)
    picked, pair_rank = group_layout(dest_all, OWN_BLK)
    my_index = lax.axis_index("grp")
    my_blocks = lax.dynamic_index_in_dim(picked, my_index, 0, keepdims=False)
    source_onehot = local_onehot(lengths[0], tokens.shape[0])
    source_totals = doc_squares(tokens, source_onehot)
    outgoing = apply_scale(tokens, source_onehot, source_totals, lengths[0], gain)
    my_dest = dest[0]
    local_index = jnp.arange(slots_in, dtype=jnp.int32)
    my_pair = jnp.sum(
        (
            (my_dest[:, None] == my_dest[None, :]) & (local_index[None, :] < local_index[:, None])
        ).astype(jnp.int32),
        axis=1,
    )
    slot_ids = jnp.arange(groups * pair_most, dtype=jnp.int32)
    send_pick = (my_dest[None, :] == (slot_ids // pair_most)[:, None]) & (
        my_pair[None, :] == (slot_ids % pair_most)[:, None]
    )
    parcel = jnp.dot(
        send_pick.astype(jnp.bfloat16),
        outgoing.reshape(slots_in, BLK * features),
        preferred_element_type=jnp.float32,
    ).astype(jnp.bfloat16)
    arrived = lax.all_to_all(parcel, "grp", split_axis=0, concat_axis=0, tiled=True)
    take_slot = my_blocks // slots_in * pair_most + pair_rank[my_blocks]
    take_onehot = (take_slot[:, None] == slot_ids[None, :]).astype(jnp.bfloat16)
    owned_rows = jnp.dot(take_onehot, arrived, preferred_element_type=jnp.float32).astype(
        jnp.bfloat16
    )
    owned_rows = owned_rows.reshape(OWN_BLK * BLK, features)
    rows_all = lax.all_gather(owned_rows, "grp", axis=0, tiled=True)
    return fold_rows(rows_all, weight)


def solution(mesh):
    placed = (
        P(("grp", "dp"), None),
        P(("grp", "dp"), None),
        P(("grp", "dp"), None),
        P(),
        P("dp", "grp"),
    )
    return jax.shard_map(
        per_device, mesh=mesh, in_specs=placed, out_specs=P("dp", "grp"), check_vma=False
    )
```

profile of v0, /device:TPU:1, one launch (start us, length us, event | category | flops | bytes accessed | tf_op | source)
XLA Modules:
  0.0 362.2 jit_solution(12504840859904070301)
XLA Ops:
  6.5 0.8 reduce-window.4
  7.4 0.6 slice.4
  8.0 0.6 iota_compare_fusion.7
  8.6 0.1 convert_reduce_fusion.2
  8.7 1.4 fusion.3
  10.1 0.1 select_reduce_fusion.2
  10.3 0.7 rsqrt_bitcast_fusion
  10.9 0.1 select_reduce_fusion.1
  11.0 1.5 fusion.5
  12.5 0.7 reshape.164
  13.2 0.2 convert_reduce_fusion.3
  13.4 2.9 fusion
  16.3 0.5 broadcast.230
  16.8 6.2 %reduce.3 = bf16[16,114688]{1,0:T(8,128)(2,1)} reduce(bf16[16,1,114688]{2,0,1:T(8,128)(2,1)} %fusion, bf16[]{:T(256)} %broadcast.230), dimensions={1}, to_apply=%copy.21.reduce_sub_computation | reduce | bytes 7340034 | tf_op jit(solution)/shard_map/all_to_all | solution.py:97
  23.0 5.9 %reshape.178 = bf16[16,2,57344]{2,1,0:T(2,128)(2,1)} reshape(bf16[16,114688]{1,0:T(8,128)(2,1)} %reduce.3) | data formatting | bytes 7340032
  28.9 15.9 %all-to-all-start = ((bf16[16,2,57344]{2,1,0:T(2,128)(2,1)}), bf16[16,2,57344]{2,1,0:T(2,128)(2,1)}, u32[]{:S(2)}, u32[]{:S(2)}) async-start(bf16[16,2,57344]{2,1,0:T(2,128)(2,1)} %reshape.178), calls=%async_computation | async-start | bytes 7340032 | tf_op jit(solution)/shard_map/all_to_all | solution.py:97
  44.9 0.0 all-gather.6.cloned.1.call-start
  44.9 0.7 all-gather.6.cloned.1.call-update
  45.7 0.1 add_bitcast_fusion
  45.7 176.0 %all-gather = s32[16,1,8]{2,1,0:T(1,128)S(1)} all-gather(s32[1,1,8]{2,1,0:T(1,128)S(1)} %add_bitcast_fusion), channel_id=1, replica_groups=mesh['grp'=16,'dp'=32] {'grp'}, dimensions={0}, use_global_device_ids=true | all-gather | bytes 544 | tf_op jit(solution)/shard_map/all_gather | solution.py:14
  221.7 0.1 copy.19
  221.8 0.1 copy.20
  221.9 0.1 eq.134
  222.0 0.2 convert_reduce_fusion.1
  222.2 0.1 select_reduce_fusion
  222.3 0.2 dynamic-slice_reduce_fusion
  222.5 0.6 gather_fusion
  223.2 12.0 %reshape.179 = bf16[16,1,114688]{2,1,0:T(2,128)(2,1)} reshape(bf16[16,2,57344]{2,1,0:T(2,128)(2,1)} %all-to-all-done) | data formatting | bytes 7340032
  235.2 7.2 %convolution_convert_fusion.1 = bf16[2,114688]{1,0:T(2,128)(2,1)S(1)} fusion(bf16[16,1,114688]{2,1,0:T(2,128)(2,1)} %reshape.179, s32[2]{0:T(128)S(1)} %fusion.17), kind=kOutput, calls=%fused_computation.3 | convolution fusion | flops 7569440 | bytes 4128776 | tf_op jit(solution)/shard_map/dot_general | solution.py:100
  242.4 1.2 reshape.165
  243.7 101.4 %all-gather.4.cloned.1.call-done = bf16[1024,3584]{1,0:T(8,128)(2,1)} async-done(((bf16[64,3584]{1,0:T(8,128)(2,1)}), bf16[1024,3584]{1,0:T(8,128)(2,1)}) %all-gather.4.cloned.1.call-update) | async-done | bytes 7340048 | tf_op jit(solution)/shard_map/all_gather | solution.py:104
  345.1 10.3 %convolution_convert_fusion.2 = bf16[1024,640]{1,0:T(8,128)(2,1)} fusion(bf16[1024,3584]{1,0:T(8,128)(2,1)} %all-gather.4.cloned.1.call-done, bf16[3584,640]{1,0:T(8,128)(2,1)} %all-gather.6.cloned.1.call-done), kind=kOutput, calls=%fused_computation.11 | convolution fusion | flops 4698275840 | bytes 13238272 | tf_op jit(solution)/shard_map/dot_general | solution.py:61
  (16 shorter events, 0.1 us)
Async XLA Ops:
  6.5 6.6 %copy-start = (s32[1,4]{1,0:T(1,128)S(1)}, s32[1,4]{1,0:T(1,128)}, u32[]{:S(2)}) copy-start(s32[1,4]{1,0:T(1,128)} %param.7) | copy-start | bytes 52
  28.9 16.7 %copy-start.1 = (s32[1,4]{1,0:T(1,128)S(1)}, s32[1,4]{1,0:T(1,128)}, u32[]{:S(2)}) copy-start(s32[1,4]{1,0:T(1,128)} %param.6) | copy-start | bytes 52
  28.9 194.3 %all-to-all-start = ((bf16[16,2,57344]{2,1,0:T(2,128)(2,1)}), bf16[16,2,57344]{2,1,0:T(2,128)(2,1)}, u32[]{:S(2)}, u32[]{:S(2)}) async-start(bf16[16,2,57344]{2,1,0:T(2,128)(2,1)} %reshape.178), calls=%async_computation | async-start | bytes 7340032 | tf_op jit(solution)/shard_map/all_to_all | solution.py:97
  44.9 198.8 %all-gather.6.cloned.1.call-start = ((), (), s32[]{:S(2)}) async-start(), calls=%async_computation.2 | async-start | bytes 4730880 | tf_op jit(solution)/shard_map/all_gather | solution.py:63
  45.6 299.5 %all-gather.4.cloned.1.call-start = ((), (), s32[]{:S(2)}) async-start(), calls=%async_computation.1 | async-start | bytes 7798784 | tf_op jit(solution)/shard_map/all_gather | solution.py:104
Sparse Core Ops, SparseCore 0:
  48.9 63.6 all-gather.5
  243.7 101.3 all-gather.3
where the time goes:
time: 363 us; the launch traced here: 362 us
  blocking collectives  176 us (48%)
  waiting for transfers between devices  102 us (28%)
  local copies, waits for them, and re-layouts  22 us (6%)
  matrix products  20.3 us (6%)
  starting transfers between devices  16 us (4%)
  between operations  13.5 us (4%)
  other arithmetic  12.2 us (3%)
    all_gather x1, blocking collectives, in_one_piece(): result = lax.all_gather(both, axis, axis=dim, tiled=True)  176 us
    all_gather x1, waiting for transfers between devices, per_device(): rows_all = lax.all_gather(owned_rows, 'grp', axis=0, tiled=True)  101 us
    unnamed x6, local copies, waits for them, and re-layouts  18 us
    all_to_all x1, starting transfers between devices, per_device(): lax.all_to_all(parcel, 'grp', split_axis=0, concat_axis=0, tiled=True)  15.9 us
    dot_general x1, matrix products, fold_rows(): jnp.dot(rows_all, lax.all_gather(weight, 'dp', axis=0, tiled=True), prefe...  10.3 us
  transfers between devices with their start and end apart: 3, of which 1 were waited for; matrix products, arithmetic and copies ran while one was open for 6% of the time, Pallas kernels for 0%

commit v1 on v0

--- a/solution.py
+++ b/solution.py
@@ -6,6 +6,28 @@
 BLK = 32
 OWN_BLK = 2
 EPS = 1e-06
+
+
+def joined_along(blocks, dim):
+    shape = list(blocks.shape[1:])
+    shape[dim] *= blocks.shape[0]
+    return jnp.moveaxis(blocks, 0, dim).reshape(shape)
+
+
+def ring_gather(x, axis, dim):
+    devices = lax.axis_size(axis)
+    pairs = [(i, (i + 1) % devices) for i in range(devices)]
+    back = [(b, a) for a, b in pairs]
+    lower, upper = ([], [])
+    for turn in range(devices - 1):
+        if turn % 2 == 0:
+            lower.append(lax.ppermute(lower[-1] if lower else x, axis, pairs))
+        else:
+            upper.append(lax.ppermute(upper[-1] if upper else x, axis, back))
+    tiles = jnp.stack([*lower[::-1], x, *upper])
+    shift = lax.axis_index(axis) - len(lower)
+    tiles = tiles[(jnp.arange(devices) - shift) % devices]
+    return joined_along(tiles, dim)
 
 
 def in_one_piece(arrays, axis, dim, along):
@@ -101,7 +123,7 @@
         jnp.bfloat16
     )
     owned_rows = owned_rows.reshape(OWN_BLK * BLK, features)
-    rows_all = lax.all_gather(owned_rows, "grp", axis=0, tiled=True)
+    rows_all = ring_gather(owned_rows, "grp", 0)
     return fold_rows(rows_all, weight)
 
 

time: 363 us -> 437 us (1.20)
  starting transfers between devices: 16 us -> 66.2 us
  local copies, waits for them, and re-layouts: 22 us -> 49.8 us
  waiting for transfers between devices: 102 us -> 95.5 us
    all_gather x1 -> x0, waiting for transfers between devices: 101 us -> none  [per_device(): rows_all = lax.all_gather(owned_rows, 'grp', axis=0, tiled=True)]
    ppermute x0 -> x15, waiting for transfers between devices: none -> 55.1 us  [the longest x8 53.3 us: ring_gather(): lower.append(lax.ppermute(lower[-1] if lower else x, axis, pairs))]
    ppermute x0 -> x15, starting transfers between devices: none -> 50.3 us  [the longest x7 34.6 us: ring_gather(): upper.append(lax.ppermute(upper[-1] if upper else x, axis, back))]
    all_gather x1, waiting for transfers between devices: 0.02 us -> 40.4 us  [fold_rows(): lax.all_gather(weight, 'dp', axis=0, tiled=True)]
    unnamed x6 -> x35, local copies, waits for them, and re-layouts: 18 us -> 38.2 us
    gather x0 -> x1, local copies, waits for them, and re-layouts: none -> 7.16 us  [ring_gather(): tiles = tiles[(jnp.arange(devices) - shift) % devices]]
  transfers between devices with their start and end apart: 3 -> 17, of which waited for: 1 -> 11; matrix products, arithmetic and copies ran while one was open for 6% -> 7% of each run, Pallas kernels for 0% -> 0%
where the time goes in v1:
time: 437 us; the launch traced here: 436 us
  blocking collectives  177 us (41%)
  waiting for transfers between devices  95.5 us (22%)
  starting transfers between devices  66.2 us (15%)
  local copies, waits for them, and re-layouts  49.8 us (11%)
  matrix products  21 us (5%)
  between operations  13.7 us (3%)
  other arithmetic  12.9 us (3%)
    all_gather x1, blocking collectives, in_one_piece(): result = lax.all_gather(both, axis, axis=dim, tiled=True)  177 us
    ppermute x8, waiting for transfers between devices, ring_gather(): lower.append(lax.ppermute(lower[-1] if lower else x, axis, pairs))  53.3 us
    all_gather x1, waiting for transfers between devices, fold_rows(): lax.all_gather(weight, 'dp', axis=0, tiled=True)  40.4 us
    unnamed x35, local copies, waits for them, and re-layouts  38.2 us
    ppermute x7, starting transfers between devices, ring_gather(): upper.append(lax.ppermute(upper[-1] if upper else x, axis, back))  34.6 us
    all_to_all x1, starting transfers between devices, per_device(): lax.all_to_all(parcel, 'grp', split_axis=0, concat_axis=0, tiled=True)  15.8 us
    ppermute x8, starting transfers between devices, ring_gather(): lower.append(lax.ppermute(lower[-1] if lower else x, axis, pairs))  15.7 us
    dot_general x1, matrix products, fold_rows(): jnp.dot(rows_all, lax.all_gather(weight, 'dp', axis=0, tiled=True), prefe...  10.3 us
  transfers between devices with their start and end apart: 17, of which 11 were waited for; matrix products, arithmetic and copies ran while one was open for 7% of the time, Pallas kernels for 0%

profile of v1, /device:TPU:1, one launch (start us, length us, event | category | flops | bytes accessed | tf_op | source)
XLA Modules:
  0.0 435.8 jit_solution(12506132122604426210)
XLA Ops:
  14.1 3.6 fusion
  18.2 6.2 %reduce.3 = bf16[16,114688]{1,0:T(8,128)(2,1)} reduce(bf16[16,1,114688]{2,0,1:T(8,128)(2,1)} %fusion, bf16[]{:T(256)} %broadcast.298), dimensions={1}, to_apply=%copy.21.reduce_sub_computation | reduce | bytes 7340034 | tf_op jit(solution)/shard_map/all_to_all | solution.py:119
  24.4 6.0 %reshape.239 = bf16[16,2,57344]{2,1,0:T(2,128)(2,1)} reshape(bf16[16,114688]{1,0:T(8,128)(2,1)} %reduce.3) | data formatting | bytes 7340032
  30.4 15.8 %all-to-all-start = ((bf16[16,2,57344]{2,1,0:T(2,128)(2,1)}), bf16[16,2,57344]{2,1,0:T(2,128)(2,1)}, u32[]{:S(2)}, u32[]{:S(2)}) async-start(bf16[16,2,57344]{2,1,0:T(2,128)(2,1)} %reshape.239), calls=%async_computation | async-start | bytes 7340032 | tf_op jit(solution)/shard_map/all_to_all | solution.py:119
  46.3 176.7 %all-gather = s32[16,1,8]{2,1,0:T(1,128)S(1)} all-gather(s32[1,1,8]{2,1,0:T(1,128)S(1)} %add_bitcast_fusion), channel_id=1, replica_groups=mesh['grp'=16,'dp'=32] {'grp'}, dimensions={0}, use_global_device_ids=true | all-gather | bytes 544 | tf_op jit(solution)/shard_map/all_gather | solution.py:36
  224.5 12.0 %reshape.240 = bf16[16,1,114688]{2,1,0:T(2,128)(2,1)} reshape(bf16[16,2,57344]{2,1,0:T(2,128)(2,1)} %all-to-all-done) | data formatting | bytes 7340032
  236.6 7.2 %convolution_convert_fusion.1 = bf16[2,114688]{1,0:T(2,128)(2,1)S(1)} fusion(bf16[16,1,114688]{2,1,0:T(2,128)(2,1)} %reshape.240, s32[2]{0:T(128)S(1)} %fusion.19), kind=kOutput, calls=%fused_computation.4 | convolution fusion | flops 7569440 | bytes 4128776 | tf_op jit(solution)/shard_map/dot_general | solution.py:122
  244.1 2.3 collective-permute-start
  246.5 8.1 %collective-permute-done = bf16[64,3584]{1,0:T(8,128)(2,1)S(1)} collective-permute-done((bf16[64,3584]{1,0:T(8,128)(2,1)S(1)}, bf16[64,3584]{1,0:T(8,128)(2,1)S(1)}, u32[]{:S(2)}, u32[]{:S(2)}) %collective-permute-start) | collective-permute-done | bytes 458784 | tf_op jit(solution)/shard_map/ppermute | solution.py:24
  254.6 1.9 collective-permute-start.1
  256.5 4.6 %collective-permute-start.8 = (bf16[64,3584]{1,0:T(8,128)(2,1)S(1)}, bf16[64,3584]{1,0:T(8,128)(2,1)S(1)}, u32[]{:S(2)}, u32[]{:S(2)}) collective-permute-start(bf16[64,3584]{1,0:T(8,128)(2,1)S(1)} %reshape.217), channel_id=1, source_target_pairs={{32,0},{64,32},{96,64},{128,96},{160,128},{192,160},{224,192},{256... | collective-permute-start | bytes 1376264 | tf_op jit(solution)/shard_map/ppermute | solution.py:26
  261.1 6.0 %collective-permute-done.1 = bf16[64,3584]{1,0:T(8,128)(2,1)S(1)} collective-permute-done((bf16[64,3584]{1,0:T(8,128)(2,1)S(1)}, bf16[64,3584]{1,0:T(8,128)(2,1)S(1)}, u32[]{:S(2)}, u32[]{:S(2)}) %collective-permute-start.1) | collective-permute-done | bytes 458784 | tf_op jit(solution)/shard_map/ppermute | solution.py:24
  269.0 4.8 %collective-permute-start.9 = (bf16[64,3584]{1,0:T(8,128)(2,1)S(1)}, bf16[64,3584]{1,0:T(8,128)(2,1)S(1)}, u32[]{:S(2)}, u32[]{:S(2)}) collective-permute-start(bf16[64,3584]{1,0:T(8,128)(2,1)S(1)} %collective-permute-done.8), channel_id=1, source_target_pairs={{32,0},{64,32},{96,64},{128,96},{160,128},{192,160},{224,192},{256... | collective-permute-start | bytes 1376264 | tf_op jit(solution)/shard_map/ppermute | solution.py:26
  273.7 6.9 %collective-permute-done.2 = bf16[64,3584]{1,0:T(8,128)(2,1)S(1)} collective-permute-done((bf16[64,3584]{1,0:T(8,128)(2,1)S(1)}, bf16[64,3584]{1,0:T(8,128)(2,1)S(1)}, u32[]{:S(2)}, u32[]{:S(2)}) %collective-permute-start.2) | collective-permute-done | bytes 458784 | tf_op jit(solution)/shard_map/ppermute | solution.py:24
  280.6 1.9 collective-permute-start.3
  282.6 4.8 %collective-permute-start.10 = (bf16[64,3584]{1,0:T(8,128)(2,1)S(1)}, bf16[64,3584]{1,0:T(8,128)(2,1)S(1)}, u32[]{:S(2)}, u32[]{:S(2)}) collective-permute-start(bf16[64,3584]{1,0:T(8,128)(2,1)S(1)} %collective-permute-done.9), channel_id=1, source_target_pairs={{32,0},{64,32},{96,64},{128,96},{160,128},{192,160},{224,192},{256... | collective-permute-start | bytes 1376264 | tf_op jit(solution)/shard_map/ppermute | solution.py:26
  287.4 8.0 %collective-permute-done.3 = bf16[64,3584]{1,0:T(8,128)(2,1)S(1)} collective-permute-done((bf16[64,3584]{1,0:T(8,128)(2,1)S(1)}, bf16[64,3584]{1,0:T(8,128)(2,1)S(1)}, u32[]{:S(2)}, u32[]{:S(2)}) %collective-permute-start.3) | collective-permute-done | bytes 458784 | tf_op jit(solution)/shard_map/ppermute | solution.py:24
  295.4 1.9 collective-permute-start.4
  297.4 5.0 %collective-permute-start.11 = (bf16[64,3584]{1,0:T(8,128)(2,1)S(1)}, bf16[64,3584]{1,0:T(8,128)(2,1)S(1)}, u32[]{:S(2)}, u32[]{:S(2)}) collective-permute-start(bf16[64,3584]{1,0:T(8,128)(2,1)S(1)} %collective-permute-done.10), channel_id=1, source_target_pairs={{32,0},{64,32},{96,64},{128,96},{160,128},{192,160},{224,192},{256... | collective-permute-start | bytes 1376264 | tf_op jit(solution)/shard_map/ppermute | solution.py:26
  302.4 8.1 %collective-permute-done.4 = bf16[64,3584]{1,0:T(8,128)(2,1)S(1)} collective-permute-done((bf16[64,3584]{1,0:T(8,128)(2,1)S(1)}, bf16[64,3584]{1,0:T(8,128)(2,1)S(1)}, u32[]{:S(2)}, u32[]{:S(2)}) %collective-permute-start.4) | collective-permute-done | bytes 458784 | tf_op jit(solution)/shard_map/ppermute | solution.py:24
  310.5 1.9 collective-permute-start.5
  313.2 4.8 %collective-permute-start.12 = (bf16[64,3584]{1,0:T(8,128)(2,1)S(1)}, bf16[64,3584]{1,0:T(8,128)(2,1)}, u32[]{:S(2)}, u32[]{:S(2)}) collective-permute-start(bf16[64,3584]{1,0:T(8,128)(2,1)S(1)} %collective-permute-done.11), channel_id=1, source_target_pairs={{32,0},{64,32},{96,64},{128,96},{160,128},{192,160},{224,192},{256... | collective-permute-start | bytes 1376264 | tf_op jit(solution)/shard_map/ppermute | solution.py:26
  318.1 6.6 %collective-permute-done.5 = bf16[64,3584]{1,0:T(8,128)(2,1)S(1)} collective-permute-done((bf16[64,3584]{1,0:T(8,128)(2,1)S(1)}, bf16[64,3584]{1,0:T(8,128)(2,1)S(1)}, u32[]{:S(2)}, u32[]{:S(2)}) %collective-permute-start.5) | collective-permute-done | bytes 458784 | tf_op jit(solution)/shard_map/ppermute | solution.py:24
  324.7 1.9 collective-permute-start.6
  327.6 5.3 %collective-permute-start.13 = (bf16[64,3584]{1,0:T(8,128)(2,1)}, bf16[64,3584]{1,0:T(8,128)(2,1)}, u32[]{:S(2)}, u32[]{:S(2)}) collective-permute-start(bf16[64,3584]{1,0:T(8,128)(2,1)} %collective-permute-done.12), channel_id=1, source_target_pairs={{32,0},{64,32},{96,64},{128,96},{160,128},{192,160},{224,192},{256... | collective-permute-start | bytes 1376264 | tf_op jit(solution)/shard_map/ppermute | solution.py:26
  332.9 5.1 %collective-permute-done.6 = bf16[64,3584]{1,0:T(8,128)(2,1)} collective-permute-done((bf16[64,3584]{1,0:T(8,128)(2,1)S(1)}, bf16[64,3584]{1,0:T(8,128)(2,1)}, u32[]{:S(2)}, u32[]{:S(2)}) %collective-permute-start.6) | collective-permute-done | bytes 458784 | tf_op jit(solution)/shard_map/ppermute | solution.py:24
  338.0 1.9 collective-permute-start.7
  341.3 5.3 %collective-permute-start.14 = (bf16[64,3584]{1,0:T(8,128)(2,1)}, bf16[64,3584]{1,0:T(8,128)(2,1)S(1)}, u32[]{:S(2)}, u32[]{:S(2)}) collective-permute-start(bf16[64,3584]{1,0:T(8,128)(2,1)} %collective-permute-done.13), channel_id=1, source_target_pairs={{32,0},{64,32},{96,64},{128,96},{160,128},{192,160},{224,192},{256... | collective-permute-start | bytes 1376264 | tf_op jit(solution)/shard_map/ppermute | solution.py:26
  346.6 4.5 %collective-permute-done.7 = bf16[64,3584]{1,0:T(8,128)(2,1)} collective-permute-done((bf16[64,3584]{1,0:T(8,128)(2,1)}, bf16[64,3584]{1,0:T(8,128)(2,1)}, u32[]{:S(2)}, u32[]{:S(2)}) %collective-permute-start.7) | collective-permute-done | bytes 458784 | tf_op jit(solution)/shard_map/ppermute | solution.py:24
  371.2 7.2 %gather_fusion.1 = bf16[16,64,3584]{2,1,0:T(8,128)(2,1)} fusion(bf16[16,64,3584]{2,1,0:T(8,128)(2,1)} %bitcast_dynamic-update-slice_fusion, s32[1024]{0:T(1024)S(1)} %pad_clamp_fusion), kind=kCustom, calls=%fused_computation.1 | custom fusion | bytes 14680128 | tf_op jit(solution)/shard_map/gather | solution.py:29
  378.3 40.4 %all-gather.3.cloned.1.call-done = bf16[3584,640]{1,0:T(8,128)(2,1)} async-done(((bf16[112,640]{1,0:T(8,128)(2,1)}), bf16[3584,640]{1,0:T(8,128)(2,1)}) %all-gather.3.cloned.1.call-update) | async-done | bytes 4587536 | tf_op jit(solution)/shard_map/all_gather | solution.py:85
  418.7 10.3 %convolution_convert_fusion.2 = bf16[1024,640]{1,0:T(8,128)(2,1)} fusion(bf16[1024,3584]{1,0:T(8,128)(2,1)} %bitcast.58, bf16[3584,640]{1,0:T(8,128)(2,1)} %all-gather.3.cloned.1.call-done), kind=kOutput, calls=%fused_computation.12 | convolution fusion | flops 4698275840 | bytes 13238272 | tf_op jit(solution)/shard_map/dot_general | solution.py:83
  (77 shorter events, 35.1 us)
Async XLA Ops:
  24.3 21.9 %copy-start.7 = (s32[1,4]{1,0:T(1,128)S(1)}, s32[1,4]{1,0:T(1,128)}, u32[]{:S(2)}) copy-start(s32[1,4]{1,0:T(1,128)} %param.7) | copy-start | bytes 52
  24.4 21.9 %copy-start.8 = (s32[1,4]{1,0:T(1,128)S(1)}, s32[1,4]{1,0:T(1,128)}, u32[]{:S(2)}) copy-start(s32[1,4]{1,0:T(1,128)} %param.6) | copy-start | bytes 52
  30.4 194.1 %all-to-all-start = ((bf16[16,2,57344]{2,1,0:T(2,128)(2,1)}), bf16[16,2,57344]{2,1,0:T(2,128)(2,1)}, u32[]{:S(2)}, u32[]{:S(2)}) async-start(bf16[16,2,57344]{2,1,0:T(2,128)(2,1)} %reshape.239), calls=%async_computation | async-start | bytes 7340032 | tf_op jit(solution)/shard_map/all_to_all | solution.py:119
  46.2 372.5 %all-gather.3.cloned.1.call-start = ((), (), s32[]{:S(2)}) async-start(), calls=%async_computation.1 | async-start | bytes 4730880 | tf_op jit(solution)/shard_map/all_gather | solution.py:85
  244.1 10.4 %collective-permute-start = (bf16[64,3584]{1,0:T(8,128)(2,1)S(1)}, bf16[64,3584]{1,0:T(8,128)(2,1)S(1)}, u32[]{:S(2)}, u32[]{:S(2)}) collective-permute-start(bf16[64,3584]{1,0:T(8,128)(2,1)S(1)} %reshape.217), channel_id=1, source_target_pairs={{0,32},{32,64},{64,96},{96,128},{128,160},{160,192},{192,224},{224... | collective-permute-start | bytes 1376264 | tf_op jit(solution)/shard_map/ppermute | solution.py:24
  254.6 12.5 %collective-permute-start.1 = (bf16[64,3584]{1,0:T(8,128)(2,1)S(1)}, bf16[64,3584]{1,0:T(8,128)(2,1)S(1)}, u32[]{:S(2)}, u32[]{:S(2)}) collective-permute-start(bf16[64,3584]{1,0:T(8,128)(2,1)S(1)} %collective-permute-done), channel_id=1, source_target_pairs={{0,32},{32,64},{64,96},{96,128},{128,160},{160,192},{192,224},{224... | collective-permute-start | bytes 1376264 | tf_op jit(solution)/shard_map/ppermute | solution.py:24
  256.5 12.5 %collective-permute-start.8 = (bf16[64,3584]{1,0:T(8,128)(2,1)S(1)}, bf16[64,3584]{1,0:T(8,128)(2,1)S(1)}, u32[]{:S(2)}, u32[]{:S(2)}) collective-permute-start(bf16[64,3584]{1,0:T(8,128)(2,1)S(1)} %reshape.217), channel_id=1, source_target_pairs={{32,0},{64,32},{96,64},{128,96},{160,128},{192,160},{224,192},{256... | collective-permute-start | bytes 1376264 | tf_op jit(solution)/shard_map/ppermute | solution.py:26
  267.0 13.6 %collective-permute-start.2 = (bf16[64,3584]{1,0:T(8,128)(2,1)S(1)}, bf16[64,3584]{1,0:T(8,128)(2,1)S(1)}, u32[]{:S(2)}, u32[]{:S(2)}) collective-permute-start(bf16[64,3584]{1,0:T(8,128)(2,1)S(1)} %collective-permute-done.1), channel_id=1, source_target_pairs={{0,32},{32,64},{64,96},{96,128},{128,160},{160,192},{192,224},{224... | collective-permute-start | bytes 1376264 | tf_op jit(solution)/shard_map/ppermute | solution.py:24
  269.0 13.6 %collective-permute-start.9 = (bf16[64,3584]{1,0:T(8,128)(2,1)S(1)}, bf16[64,3584]{1,0:T(8,128)(2,1)S(1)}, u32[]{:S(2)}, u32[]{:S(2)}) collective-permute-start(bf16[64,3584]{1,0:T(8,128)(2,1)S(1)} %collective-permute-done.8), channel_id=1, source_target_pairs={{32,0},{64,32},{96,64},{128,96},{160,128},{192,160},{224,192},{256... | collective-permute-start | bytes 1376264 | tf_op jit(solution)/shard_map/ppermute | solution.py:26
  280.6 14.8 %collective-permute-start.3 = (bf16[64,3584]{1,0:T(8,128)(2,1)S(1)}, bf16[64,3584]{1,0:T(8,128)(2,1)S(1)}, u32[]{:S(2)}, u32[]{:S(2)}) collective-permute-start(bf16[64,3584]{1,0:T(8,128)(2,1)S(1)} %collective-permute-done.2), channel_id=1, source_target_pairs={{0,32},{32,64},{64,96},{96,128},{128,160},{160,192},{192,224},{224... | collective-permute-start | bytes 1376264 | tf_op jit(solution)/shard_map/ppermute | solution.py:24
  282.6 14.8 %collective-permute-start.10 = (bf16[64,3584]{1,0:T(8,128)(2,1)S(1)}, bf16[64,3584]{1,0:T(8,128)(2,1)S(1)}, u32[]{:S(2)}, u32[]{:S(2)}) collective-permute-start(bf16[64,3584]{1,0:T(8,128)(2,1)S(1)} %collective-permute-done.9), channel_id=1, source_target_pairs={{32,0},{64,32},{96,64},{128,96},{160,128},{192,160},{224,192},{256... | collective-permute-start | bytes 1376264 | tf_op jit(solution)/shard_map/ppermute | solution.py:26
  295.4 32.2 %copy-start.4 = (bf16[64,3584]{1,0:T(8,128)(2,1)}, bf16[64,3584]{1,0:T(8,128)(2,1)S(1)}, u32[]{:S(2)}) copy-start(bf16[64,3584]{1,0:T(8,128)(2,1)S(1)} %collective-permute-done.3) | copy-start | bytes 1376260
  295.4 15.1 %collective-permute-start.4 = (bf16[64,3584]{1,0:T(8,128)(2,1)S(1)}, bf16[64,3584]{1,0:T(8,128)(2,1)S(1)}, u32[]{:S(2)}, u32[]{:S(2)}) collective-permute-start(bf16[64,3584]{1,0:T(8,128)(2,1)S(1)} %collective-permute-done.3), channel_id=1, source_target_pairs={{0,32},{32,64},{64,96},{96,128},{128,160},{160,192},{192,224},{224... | collective-permute-start | bytes 1376264 | tf_op jit(solution)/shard_map/ppermute | solution.py:24
  297.3 42.7 %copy-start = (bf16[64,3584]{1,0:T(8,128)(2,1)}, bf16[64,3584]{1,0:T(8,128)(2,1)S(1)}, u32[]{:S(2)}) copy-start(bf16[64,3584]{1,0:T(8,128)(2,1)S(1)} %collective-permute-done.10) | copy-start | bytes 1376260
  297.4 15.0 %collective-permute-start.11 = (bf16[64,3584]{1,0:T(8,128)(2,1)S(1)}, bf16[64,3584]{1,0:T(8,128)(2,1)S(1)}, u32[]{:S(2)}, u32[]{:S(2)}) collective-permute-start(bf16[64,3584]{1,0:T(8,128)(2,1)S(1)} %collective-permute-done.10), channel_id=1, source_target_pairs={{32,0},{64,32},{96,64},{128,96},{160,128},{192,160},{224,192},{256... | collective-permute-start | bytes 1376264 | tf_op jit(solution)/shard_map/ppermute | solution.py:26
  310.5 22.4 %copy-start.5 = (bf16[64,3584]{1,0:T(8,128)(2,1)}, bf16[64,3584]{1,0:T(8,128)(2,1)S(1)}, u32[]{:S(2)}) copy-start(bf16[64,3584]{1,0:T(8,128)(2,1)S(1)} %collective-permute-done.4) | copy-start | bytes 1376260
  310.5 14.2 %collective-permute-start.5 = (bf16[64,3584]{1,0:T(8,128)(2,1)S(1)}, bf16[64,3584]{1,0:T(8,128)(2,1)S(1)}, u32[]{:S(2)}, u32[]{:S(2)}) collective-permute-start(bf16[64,3584]{1,0:T(8,128)(2,1)S(1)} %collective-permute-done.4), channel_id=1, source_target_pairs={{0,32},{32,64},{64,96},{96,128},{128,160},{160,192},{192,224},{224... | collective-permute-start | bytes 1376264 | tf_op jit(solution)/shard_map/ppermute | solution.py:24
  312.4 0.8 copy-start.2
  313.2 14.4 %collective-permute-start.12 = (bf16[64,3584]{1,0:T(8,128)(2,1)S(1)}, bf16[64,3584]{1,0:T(8,128)(2,1)}, u32[]{:S(2)}, u32[]{:S(2)}) collective-permute-start(bf16[64,3584]{1,0:T(8,128)(2,1)S(1)} %collective-permute-done.11), channel_id=1, source_target_pairs={{32,0},{64,32},{96,64},{128,96},{160,128},{192,160},{224,192},{256... | collective-permute-start | bytes 1376264 | tf_op jit(solution)/shard_map/ppermute | solution.py:26
  324.7 13.4 %copy-start.6 = (bf16[64,3584]{1,0:T(8,128)(2,1)}, bf16[64,3584]{1,0:T(8,128)(2,1)S(1)}, u32[]{:S(2)}) copy-start(bf16[64,3584]{1,0:T(8,128)(2,1)S(1)} %collective-permute-done.5) | copy-start | bytes 1376260
  324.7 13.4 %collective-permute-start.6 = (bf16[64,3584]{1,0:T(8,128)(2,1)S(1)}, bf16[64,3584]{1,0:T(8,128)(2,1)}, u32[]{:S(2)}, u32[]{:S(2)}) collective-permute-start(bf16[64,3584]{1,0:T(8,128)(2,1)S(1)} %collective-permute-done.5), channel_id=1, source_target_pairs={{0,32},{32,64},{64,96},{96,128},{128,160},{160,192},{192,224},{224... | collective-permute-start | bytes 1376264 | tf_op jit(solution)/shard_map/ppermute | solution.py:24
  327.6 13.7 %collective-permute-start.13 = (bf16[64,3584]{1,0:T(8,128)(2,1)}, bf16[64,3584]{1,0:T(8,128)(2,1)}, u32[]{:S(2)}, u32[]{:S(2)}) collective-permute-start(bf16[64,3584]{1,0:T(8,128)(2,1)} %collective-permute-done.12), channel_id=1, source_target_pairs={{32,0},{64,32},{96,64},{128,96},{160,128},{192,160},{224,192},{256... | collective-permute-start | bytes 1376264 | tf_op jit(solution)/shard_map/ppermute | solution.py:26
  338.0 13.0 %collective-permute-start.7 = (bf16[64,3584]{1,0:T(8,128)(2,1)}, bf16[64,3584]{1,0:T(8,128)(2,1)}, u32[]{:S(2)}, u32[]{:S(2)}) collective-permute-start(bf16[64,3584]{1,0:T(8,128)(2,1)} %collective-permute-done.6), channel_id=1, source_target_pairs={{0,32},{32,64},{64,96},{96,128},{128,160},{160,192},{192,224},{224... | collective-permute-start | bytes 1376264 | tf_op jit(solution)/shard_map/ppermute | solution.py:24
  340.5 24.6 %copy-start.1 = (bf16[64,3584]{1,0:T(8,128)(2,1)S(1)}, bf16[64,3584]{1,0:T(8,128)(2,1)}, u32[]{:S(2)}) copy-start(bf16[64,3584]{1,0:T(8,128)(2,1)} %copy-done) | copy-start | bytes 1376260
  340.5 25.4 %copy-start.3 = (bf16[64,3584]{1,0:T(8,128)(2,1)S(1)}, bf16[64,3584]{1,0:T(8,128)(2,1)}, u32[]{:S(2)}) copy-start(bf16[64,3584]{1,0:T(8,128)(2,1)} %copy-done.2) | copy-start | bytes 1376260
  341.3 29.1 %collective-permute-start.14 = (bf16[64,3584]{1,0:T(8,128)(2,1)}, bf16[64,3584]{1,0:T(8,128)(2,1)S(1)}, u32[]{:S(2)}, u32[]{:S(2)}) collective-permute-start(bf16[64,3584]{1,0:T(8,128)(2,1)} %collective-permute-done.13), channel_id=1, source_target_pairs={{32,0},{64,32},{96,64},{128,96},{160,128},{192,160},{224,192},{256... | collective-permute-start | bytes 1376264 | tf_op jit(solution)/shard_map/ppermute | solution.py:26
Sparse Core Ops, SparseCore 0:
  340.1 78.5 all-gather.2
